TPU v7x, 32 devices: a whole 2x2x4 slice. The times are simulated.
32 devices in a mesh: section: 2 (over core), fsdp: 4 (over y, x), tp: 4 (over z).
Axes of the slice: x: 2, y: 2, z: 4, core: 2. Of those that a mesh axis runs over, the one named last changes fastest.
Arguments:
- saved_inputs: bfloat16 [2, 8, 256, 2560], P('section', None, 'fsdp', 'tp'), may hold values from -6 to 6
- top_grad: bfloat16 [8, 256, 2560], P(None, 'fsdp', 'tp'), may hold values from -6 to 6
- norm_gain: float32 [2, 2560], P('section'), may hold values from 0.5 to 1.5
- gate_weight: bfloat16 [2, 2560, 6912], P('section', 'fsdp', 'tp'), may hold values from -0.125 to 0.125
- up_weight: bfloat16 [2, 2560, 6912], P('section', 'fsdp', 'tp'), may hold values from -0.125 to 0.125
- down_weight: bfloat16 [2, 6912, 2560], P('section', 'tp', 'fsdp'), may hold values from -0.078125 to 0.078125
Outputs:
- input_grads: bfloat16 [2, 8, 256, 2560], P('section', None, 'fsdp', 'tp')
- gate_grad: float32 [2, 2560, 6912], P('section', 'fsdp', 'tp')
- up_grad: float32 [2, 2560, 6912], P('section', 'fsdp', 'tp')
- down_grad: float32 [2, 6912, 2560], P('section', 'tp', 'fsdp')
- gain_grad: float32 [2, 2560], P('section', 'tp')
All inputs are finite; a program needn't handle non-finite values.
Results may differ from a plain program's by a relative error of at most 0.0055.
Values may be sent and summed in bfloat16 or wider, within the bound.
A program may use at most 192 MiB of HBM per device.

v0:
```python
import jax
import jax.numpy as jnp
from jax import lax
from jax.sharding import PartitionSpec as P

epsilon = 1e-05


def for_sending(x):

    def short(part):
        return part.astype(jnp.bfloat16) if part.dtype == jnp.float32 else part

    return jax.tree.map(short, x)


def passed_along(block, axis, distance):
    devices = range(lax.axis_size(axis))
    route = [(i - distance, i) for i in devices if i - distance in devices]
    return lax.ppermute(block, axis, route)


def select_micro(buffer, micro_index):
    return lax.dynamic_index_in_dim(buffer, micro_index, 0, keepdims=False)


def store_micro(buffer, micro_index, update, condition):
    previous = select_micro(buffer, micro_index)
    return lax.dynamic_update_index_in_dim(
        buffer, jnp.where(condition, update, previous), micro_index, 0
    )


def contract_rows(left, right):
    return lax.dot_general(
        left, right, (((0,), (0,)), ((), ())), preferred_element_type=jnp.float32
    )


def contract_cols(left, right):
    return lax.dot_general(
        left, right, (((1,), (1,)), ((), ())), preferred_element_type=jnp.float32
    )


def shards(saved_inputs, top_grad, norm_gain, gate_weight, up_weight, down_weight):
    section_count = lax.axis_size("section")
    section_index = lax.axis_index("section")
    tp_count = lax.axis_size("tp")
    micro_count = saved_inputs.shape[1]
    row_count = saved_inputs.shape[2]
    local_width = saved_inputs.shape[3]
    full_width = local_width * tp_count
    w_gate, w_up, w_down = (
        lax.all_gather(gate_weight[0], "fsdp", axis=0, tiled=True),
        lax.all_gather(up_weight[0], "fsdp", axis=0, tiled=True),
        lax.all_gather(down_weight[0], "fsdp", axis=1, tiled=True),
    )
    hidden_width = w_gate.shape[1]
    gain_full = norm_gain[0]
    column_start = lax.axis_index("tp") * local_width
    gain_local = lax.dynamic_slice_in_dim(gain_full, column_start, local_width)
    inputs_local = saved_inputs[0]
    inputs_full = lax.all_gather(inputs_local, "tp", axis=2, tiled=True)
    inputs_wide = inputs_full.astype(jnp.float32)
    row_scale = lax.rsqrt(jnp.mean(inputs_wide * inputs_wide, axis=-1, keepdims=True) + epsilon)
    normed = (inputs_wide * row_scale * gain_full).astype(jnp.bfloat16)
    gate_pre = jnp.einsum("mtd,df->mtf", normed, w_gate, preferred_element_type=jnp.float32)
    upward = jnp.einsum("mtd,df->mtf", normed, w_up, preferred_element_type=jnp.float32)
    gate_sigmoid = jax.nn.sigmoid(gate_pre)
    silu_out = gate_pre * gate_sigmoid
    hidden = (silu_out * upward).astype(jnp.bfloat16)
    last_section = section_index == section_count - 1

    def one_tick(tick_number, loop_state):
        received, grads_out, gain_total, stored = loop_state
        micro_raw = tick_number - (section_count - 1 - section_index)
        is_valid = (micro_raw >= 0) & (micro_raw < micro_count)
        micro_index = jnp.clip(micro_raw, 0, micro_count - 1)
        top_piece = select_micro(top_grad, micro_index)
        cotangent = jnp.where(last_section, top_piece, received)
        full_cotangent = lax.all_gather(for_sending(cotangent), "tp", axis=1, tiled=True).astype(
            cotangent.dtype
        )
        gate_now = select_micro(gate_pre, micro_index)
        upward_now = select_micro(upward, micro_index)
        sigmoid_now = select_micro(gate_sigmoid, micro_index)
        silu_now = select_micro(silu_out, micro_index)
        d_hidden = contract_cols(full_cotangent, w_down)
        d_gate = (
            d_hidden * upward_now * sigmoid_now * (1.0 + gate_now * (1.0 - sigmoid_now))
        ).astype(jnp.bfloat16)
        d_up = (d_hidden * silu_now).astype(jnp.bfloat16)
        partial_value = contract_cols(d_gate, w_gate) + contract_cols(d_up, w_up)
        scale_now = select_micro(row_scale, micro_index)
        unit_local = select_micro(inputs_local, micro_index).astype(jnp.float32) * scale_now
        unit_full = select_micro(inputs_wide, micro_index) * scale_now
        d_normed_full = lax.psum(partial_value, "tp")
        norm_stat = jnp.mean(d_normed_full * gain_full * unit_full, axis=-1, keepdims=True)
        d_normed = lax.dynamic_slice_in_dim(d_normed_full, column_start, local_width, 1)
        scaled = d_normed * gain_local
        d_inputs = (
            cotangent.astype(jnp.float32) + scale_now * (scaled - unit_local * norm_stat)
        ).astype(jnp.bfloat16)
        grads_out = store_micro(grads_out, micro_index, d_inputs, is_valid)
        valid_float = is_valid.astype(jnp.float32)
        gain_total = gain_total + valid_float * jnp.sum(d_normed * unit_local, axis=0)
        valid_weight = is_valid.astype(jnp.bfloat16)
        normed_now = select_micro(normed, micro_index)
        hidden_now = select_micro(hidden, micro_index)
        stored = (
            stored[0] + contract_rows(normed_now, d_gate * valid_weight),
            stored[1] + contract_rows(normed_now, d_up * valid_weight),
            stored[2] + contract_rows(full_cotangent * valid_weight, hidden_now),
        )
        handed = passed_along(d_inputs, "section", -1)
        return (handed, grads_out, gain_total, stored)

    stored_init = (
        jnp.zeros((full_width, hidden_width), jnp.float32),
        jnp.zeros((full_width, hidden_width), jnp.float32),
        jnp.zeros((full_width, hidden_width), jnp.float32),
    )
    initial = (
        jnp.zeros((row_count, local_width), jnp.bfloat16),
        jnp.zeros((micro_count, row_count, local_width), jnp.bfloat16),
        jnp.zeros((local_width,), jnp.float32),
        stored_init,
    )
    handed_last, grads_out, gain_total, stored = lax.fori_loop(
        0, micro_count + section_count - 1, one_tick, initial
    )
    gate_share, up_share, down_share = (
        lax.psum_scatter(stored[0], "fsdp", scatter_dimension=0, tiled=True),
        lax.psum_scatter(stored[1], "fsdp", scatter_dimension=0, tiled=True),
        lax.psum_scatter(stored[2], "fsdp", scatter_dimension=0, tiled=True),
    )
    gain_share = lax.psum(gain_total, "fsdp")
    return (grads_out[None], gate_share[None], up_share[None], down_share.T[None], gain_share[None])


def solution(mesh):
    placed = (
        P("section", None, "fsdp", "tp"),
        P(None, "fsdp", "tp"),
        P("section", None),
        P("section", "fsdp", "tp"),
        P("section", "fsdp", "tp"),
        P("section", "tp", "fsdp"),
    )
    return jax.shard_map(
        shards,
        mesh=mesh,
        in_specs=placed,
        out_specs=(
            P("section", None, "fsdp", "tp"),
            P("section", "fsdp", "tp"),
            P("section", "fsdp", "tp"),
            P("section", "tp", "fsdp"),
            P("section", "tp"),
        ),
        check_vma=False,
    )
```

profile of v0, /device:TPU:0, one launch (start us, length us, event | category | flops | bytes accessed | tf_op | source)
XLA Modules:
  0.0 1582.6 jit_solution(9711850092869869036)
XLA Ops:
  10.1 56.8 %all-gather.9.cloned.1.call-done = bf16[1,8,64,2560]{3,2,1,0:T(8,128)(2,1)} async-done(((bf16[1,8,64,640]{3,2,1,0:T(8,128)(2,1)}), bf16[1,8,64,2560]{3,2,1,0:T(8,128)(2,1)}) %all-gather.9.cloned.1.call-update) | async-done | bytes 2621456 | tf_op jit(solution)/shard_map/all_gather | solution.py:64
  75.1 83.7 %all-gather.13.cloned.1.call-done = bf16[1,2560,1728]{1,2,0:T(8,128)(2,1)} async-done(((bf16[1,640,1728]{1,2,0:T(8,128)(2,1)}), bf16[1,2560,1728]{1,2,0:T(8,128)(2,1)}) %all-gather.13.cloned.1.call-update) | async-done | bytes 8847376 | tf_op jit(solution)/shard_map/all_gather | solution.py:56
  158.8 13.1 copy.12
  171.8 80.1 %all-gather.15.cloned.1.call-done = bf16[1,2560,1728]{1,2,0:T(8,128)(2,1)} async-done(((bf16[1,640,1728]{1,2,0:T(8,128)(2,1)}), bf16[1,2560,1728]{1,2,0:T(8,128)(2,1)}) %all-gather.15.cloned.1.call-update) | async-done | bytes 8847376 | tf_op jit(solution)/shard_map/all_gather | solution.py:55
  251.9 13.1 copy.11
  274.4 11.5 multiply_convert_fusion.1
  285.9 59.1 %all-gather.11.cloned.1.call-done = bf16[1,1728,2560]{2,1,0:T(8,128)(2,1)} async-done(((bf16[1,1728,640]{2,1,0:T(8,128)(2,1)}), bf16[1,1728,2560]{2,1,0:T(8,128)(2,1)}) %all-gather.11.cloned.1.call-update) | async-done | bytes 8847376 | tf_op jit(solution)/shard_map/all_gather | solution.py:57
  345.9 734.4 %while.26 = (s32[]{:T(128)}, bf16[64,640]{1,0:T(8,128)(2,1)S(1)}, bf16[8,64,640]{2,1,0:T(8,128)(2,1)}, f32[640]{0:T(1024)S(1)}, f32[2560,1728]{0,1:T(8,128)}, /*...) while((s32[]{:T(128)}, bf16[64,640]{1,0:T(8,128)(2,1)S(1)}, ...), condition=%wide.region_5.6_spmd.clone, body=%wide.region_1.5_spmd.clone.sunk | while | flops 3426907392 | bytes 217691936 | solution.py:130
  346.8 14.2 all_gather.27
  376.7 9.6 select_add_fusion.11
  394.8 8.6 select_add_fusion.9
  403.4 13.2 all-reduce.2.cloned.1.call-done
  423.9 14.4 all_gather.27
  454.1 14.9 select_add_fusion.11
  469.0 14.6 select_add_fusion.10
  483.6 14.7 select_add_fusion.9
  505.7 14.4 all_gather.27
  535.8 14.9 select_add_fusion.11
  550.7 14.6 select_add_fusion.10
  565.4 14.7 select_add_fusion.9
  587.4 14.4 all_gather.27
  617.6 14.9 select_add_fusion.11
  632.5 14.7 select_add_fusion.10
  647.2 14.7 select_add_fusion.9
  669.2 14.7 all_gather.27
  699.6 14.9 select_add_fusion.11
  714.5 14.7 select_add_fusion.10
  729.2 14.7 select_add_fusion.9
  751.3 15.1 all_gather.27
  782.1 14.9 select_add_fusion.11
  797.0 14.7 select_add_fusion.10
  811.7 14.7 select_add_fusion.9
  833.7 15.1 all_gather.27
  864.6 14.9 select_add_fusion.11
  879.5 14.7 select_add_fusion.10
  894.2 14.7 select_add_fusion.9
  916.2 15.1 all_gather.27
  947.0 14.9 select_add_fusion.11
  962.0 14.7 select_add_fusion.10
  976.6 14.7 select_add_fusion.9
  998.7 15.1 all_gather.27
  1029.5 14.9 select_add_fusion.11
  1044.4 14.7 select_add_fusion.10
  1059.1 14.7 select_add_fusion.9
  1082.0 9.5 psum.20
  1091.5 155.1 %reduce-scatter.6.cloned.1.call-done = f32[640,1728]{0,1:T(8,128)} async-done(((f32[2560,1728]{0,1:T(8,128)}), f32[640,1728]{0,1:T(8,128)}) %reduce-scatter.6.cloned.1.call-update) | async-done | bytes 4423696 | tf_op jit(solution)/shard_map/reduce_scatter | solution.py:135
  1246.5 164.8 %reduce-scatter.8.cloned.1.call-done = f32[640,1728]{0,1:T(8,128)} async-done(((f32[2560,1728]{0,1:T(8,128)}), f32[640,1728]{0,1:T(8,128)}) %reduce-scatter.8.cloned.1.call-update) | async-done | bytes 4423696 | tf_op jit(solution)/shard_map/reduce_scatter | solution.py:136
  1411.3 164.8 %reduce-scatter.4.cloned.1.call-done = f32[640,1728]{0,1:T(8,128)} async-done(((f32[2560,1728]{0,1:T(8,128)}), f32[640,1728]{0,1:T(8,128)}) %reduce-scatter.4.cloned.1.call-update) | async-done | bytes 4423696 | tf_op jit(solution)/shard_map/reduce_scatter | solution.py:134
  (241 shorter events, 238.4 us)
Async XLA Ops:
  7.2 59.7 %all-gather.9.cloned.1.call-start = ((), (), s32[]{:S(2)}) async-start(), calls=%async_computation.6 | async-start | bytes 3276800 | tf_op jit(solution)/shard_map/all_gather | solution.py:64
  7.9 150.8 %all-gather.13.cloned.1.call-start = ((), (), s32[]{:S(2)}) async-start(), calls=%async_computation.8 | async-start | bytes 11059200 | tf_op jit(solution)/shard_map/all_gather | solution.py:56
  8.7 243.3 %all-gather.15.cloned.1.call-start = ((), (), s32[]{:S(2)}) async-start(), calls=%async_computation.9 | async-start | bytes 11059200 | tf_op jit(solution)/shard_map/all_gather | solution.py:55
  9.4 335.6 %all-gather.11.cloned.1.call-start = ((), (), s32[]{:S(2)}) async-start(), calls=%async_computation.7 | async-start | bytes 11059200 | tf_op jit(solution)/shard_map/all_gather | solution.py:57
  66.9 4.9 copy-start.2
  345.9 70.7 %all-reduce.2.cloned.1.call-start = ((), (), s32[]{:S(2)}) async-start(), calls=%async_computation.10 | async-start | bytes 1310720 | tf_op jit(solution)/shard_map/while/body/eval_jaxpr/psum | solution.py:98
  361.0 6.9 copy-start
  394.8 23.3 %copy-start.3 = (bf16[1,64,640]{2,1,0:T(8,128)(2,1)S(1)}, bf16[1,64,640]{2,1,0:T(8,128)(2,1)}, u32[]{:S(2)}) copy-start(bf16[1,64,640]{2,1,0:T(8,128)(2,1)} %constant_dynamic-slice_fusion.3) | copy-start | bytes 245764 | tf_op jit(solution)/shard_map/while
  419.9 3.2 collective-permute-start
  423.0 75.3 %all-reduce.2.cloned.1.call-start = ((), (), s32[]{:S(2)}) async-start(), calls=%async_computation.10 | async-start | bytes 1310720 | tf_op jit(solution)/shard_map/while/body/eval_jaxpr/psum | solution.py:98
  438.3 6.9 copy-start
  483.6 16.2 %copy-start.3 = (bf16[1,64,640]{2,1,0:T(8,128)(2,1)S(1)}, bf16[1,64,640]{2,1,0:T(8,128)(2,1)}, u32[]{:S(2)}) copy-start(bf16[1,64,640]{2,1,0:T(8,128)(2,1)} %constant_dynamic-slice_fusion.3) | copy-start | bytes 245764 | tf_op jit(solution)/shard_map/while
  501.6 3.2 collective-permute-start
  504.8 75.3 %all-reduce.2.cloned.1.call-start = ((), (), s32[]{:S(2)}) async-start(), calls=%async_computation.10 | async-start | bytes 1310720 | tf_op jit(solution)/shard_map/while/body/eval_jaxpr/psum | solution.py:98
  520.1 6.8 copy-start
  526.9 3.6 copy-start.1
  565.4 16.2 %copy-start.3 = (bf16[1,64,640]{2,1,0:T(8,128)(2,1)S(1)}, bf16[1,64,640]{2,1,0:T(8,128)(2,1)}, u32[]{:S(2)}) copy-start(bf16[1,64,640]{2,1,0:T(8,128)(2,1)} %constant_dynamic-slice_fusion.3) | copy-start | bytes 245764 | tf_op jit(solution)/shard_map/while
  583.4 3.2 collective-permute-start
  586.5 75.3 %all-reduce.2.cloned.1.call-start = ((), (), s32[]{:S(2)}) async-start(), calls=%async_computation.10 | async-start | bytes 1310720 | tf_op jit(solution)/shard_map/while/body/eval_jaxpr/psum | solution.py:98
  601.8 6.8 copy-start
  608.6 3.6 copy-start.1
  647.2 16.2 %copy-start.3 = (bf16[1,64,640]{2,1,0:T(8,128)(2,1)S(1)}, bf16[1,64,640]{2,1,0:T(8,128)(2,1)}, u32[]{:S(2)}) copy-start(bf16[1,64,640]{2,1,0:T(8,128)(2,1)} %constant_dynamic-slice_fusion.3) | copy-start | bytes 245764 | tf_op jit(solution)/shard_map/while
  665.1 3.2 collective-permute-start
  668.3 75.6 %all-reduce.2.cloned.1.call-start = ((), (), s32[]{:S(2)}) async-start(), calls=%async_computation.10 | async-start | bytes 1310720 | tf_op jit(solution)/shard_map/while/body/eval_jaxpr/psum | solution.py:98
  683.9 6.8 copy-start
  690.7 3.6 copy-start.1
  729.2 16.2 %copy-start.3 = (bf16[1,64,640]{2,1,0:T(8,128)(2,1)S(1)}, bf16[1,64,640]{2,1,0:T(8,128)(2,1)}, u32[]{:S(2)}) copy-start(bf16[1,64,640]{2,1,0:T(8,128)(2,1)} %constant_dynamic-slice_fusion.3) | copy-start | bytes 245764 | tf_op jit(solution)/shard_map/while
  747.2 3.2 collective-permute-start
  750.3 76.0 %all-reduce.2.cloned.1.call-start = ((), (), s32[]{:S(2)}) async-start(), calls=%async_computation.10 | async-start | bytes 1310720 | tf_op jit(solution)/shard_map/while/body/eval_jaxpr/psum | solution.py:98
  766.3 6.8 copy-start
  811.7 16.2 %copy-start.3 = (bf16[1,64,640]{2,1,0:T(8,128)(2,1)S(1)}, bf16[1,64,640]{2,1,0:T(8,128)(2,1)}, u32[]{:S(2)}) copy-start(bf16[1,64,640]{2,1,0:T(8,128)(2,1)} %constant_dynamic-slice_fusion.3) | copy-start | bytes 245764 | tf_op jit(solution)/shard_map/while
  829.7 3.2 collective-permute-start
  832.8 76.0 %all-reduce.2.cloned.1.call-start = ((), (), s32[]{:S(2)}) async-start(), calls=%async_computation.10 | async-start | bytes 1310720 | tf_op jit(solution)/shard_map/while/body/eval_jaxpr/psum | solution.py:98
  848.8 6.8 copy-start
  894.2 16.2 %copy-start.3 = (bf16[1,64,640]{2,1,0:T(8,128)(2,1)S(1)}, bf16[1,64,640]{2,1,0:T(8,128)(2,1)}, u32[]{:S(2)}) copy-start(bf16[1,64,640]{2,1,0:T(8,128)(2,1)} %constant_dynamic-slice_fusion.3) | copy-start | bytes 245764 | tf_op jit(solution)/shard_map/while
  912.1 3.2 collective-permute-start
  915.3 76.0 %all-reduce.2.cloned.1.call-start = ((), (), s32[]{:S(2)}) async-start(), calls=%async_computation.10 | async-start | bytes 1310720 | tf_op jit(solution)/shard_map/while/body/eval_jaxpr/psum | solution.py:98
  931.3 6.8 copy-start
  976.6 16.2 %copy-start.3 = (bf16[1,64,640]{2,1,0:T(8,128)(2,1)S(1)}, bf16[1,64,640]{2,1,0:T(8,128)(2,1)}, u32[]{:S(2)}) copy-start(bf16[1,64,640]{2,1,0:T(8,128)(2,1)} %constant_dynamic-slice_fusion.3) | copy-start | bytes 245764 | tf_op jit(solution)/shard_map/while
  994.6 3.2 collective-permute-start
  997.8 76.0 %all-reduce.2.cloned.1.call-start = ((), (), s32[]{:S(2)}) async-start(), calls=%async_computation.10 | async-start | bytes 1310720 | tf_op jit(solution)/shard_map/while/body/eval_jaxpr/psum | solution.py:98
  1013.8 6.8 copy-start
  1020.6 3.6 copy-start.1
  1059.1 16.2 %copy-start.3 = (bf16[1,64,640]{2,1,0:T(8,128)(2,1)S(1)}, bf16[1,64,640]{2,1,0:T(8,128)(2,1)}, u32[]{:S(2)}) copy-start(bf16[1,64,640]{2,1,0:T(8,128)(2,1)} %constant_dynamic-slice_fusion.3) | copy-start | bytes 245764 | tf_op jit(solution)/shard_map/while
  1077.1 3.2 collective-permute-start
  1080.2 166.3 %reduce-scatter.6.cloned.1.call-start = ((), (), s32[]{:S(2)}) async-start(), calls=%async_computation.4 | async-start | bytes 22118400 | tf_op jit(solution)/shard_map/reduce_scatter | solution.py:135
  1080.8 330.5 %reduce-scatter.8.cloned.1.call-start = ((), (), s32[]{:S(2)}) async-start(), calls=%async_computation.5 | async-start | bytes 22118400 | tf_op jit(solution)/shard_map/reduce_scatter | solution.py:136
  1081.4 494.7 %reduce-scatter.4.cloned.1.call-start = ((), (), s32[]{:S(2)}) async-start(), calls=%async_computation.3 | async-start | bytes 22118400 | tf_op jit(solution)/shard_map/reduce_scatter | solution.py:134
  (7 other events, 22.7 us)
Sparse Core Ops, SparseCore 0:
  9.6 57.2 all-gather.8
  68.7 89.9 all-gather.12
  160.6 91.2 all-gather.14
  253.6 91.2 all-gather.10
  375.3 41.2 all-reduce.1
  452.6 40.0 all-reduce.1
  534.3 40.3 all-reduce.1
  616.1 40.8 all-reduce.1
  698.1 41.2 all-reduce.1
  780.6 41.2 all-reduce.1
  863.1 41.1 all-reduce.1
  945.6 41.1 all-reduce.1
  1028.0 41.1 all-reduce.1
  1084.4 162.0 reduce-scatter.5
  1250.1 161.1 reduce-scatter.7
  1414.9 161.1 reduce-scatter.3
where the time goes:
time: 1590 us; the launch traced here: 1580 us
  waiting for transfers between devices  789 us (50%)
  matrix products  520 us (33%)
  blocking collectives  142 us (9%)
  other arithmetic  55.5 us (3%)
  local copies, waits for them, and re-layouts  49.3 us (3%)
    dot_general x27, matrix products, contract_rows(): lax.dot_general(left, right, (((0,), (0,)), ((), ())), preferred_element_...  381 us
    reduce_scatter x1, waiting for transfers between devices, shards(): lax.psum_scatter(stored[0], 'fsdp', scatter_dimension=0, tiled=True)  165 us
    reduce_scatter x1, waiting for transfers between devices, shards(): lax.psum_scatter(stored[2], 'fsdp', scatter_dimension=0, tiled=True)  165 us
    reduce_scatter x1, waiting for transfers between devices, shards(): lax.psum_scatter(stored[1], 'fsdp', scatter_dimension=0, tiled=True)  155 us
    all_gather x9, blocking collectives, one_tick(): lax.all_gather(for_sending(cotangent), 'tp', axis=1, tiled=True)  132 us
    dot_general x27, matrix products, contract_cols(): lax.dot_general(left, right, (((1,), (1,)), ((), ())), preferred_element_...  121 us
    all_gather x1, waiting for transfers between devices, shards(): lax.all_gather(up_weight[0], 'fsdp', axis=0, tiled=True)  83.7 us
    all_gather x1, waiting for transfers between devices, shards(): lax.all_gather(gate_weight[0], 'fsdp', axis=0, tiled=True)  80.1 us
  transfers between devices with their start and end apart: 25, of which 17 were waited for; matrix products, arithmetic and copies ran while one was open for 29% of the time, Pallas kernels for 0%

commit v1 on v0

--- a/solution.py
+++ b/solution.py
@@ -4,6 +4,9 @@
 from jax.sharding import PartitionSpec as P
 
 epsilon = 1e-05
+close_slices_over_axis = lambda frame_in, dimension_no: jnp.concatenate(
+    jax.lax.all_gather(frame_in, "tp"), dimension_no
+)
 
 
 def for_sending(x):
@@ -79,9 +82,7 @@
         micro_index = jnp.clip(micro_raw, 0, micro_count - 1)
         top_piece = select_micro(top_grad, micro_index)
         cotangent = jnp.where(last_section, top_piece, received)
-        full_cotangent = lax.all_gather(for_sending(cotangent), "tp", axis=1, tiled=True).astype(
-            cotangent.dtype
-        )
+        full_cotangent = close_slices_over_axis(for_sending(cotangent), 1).astype(cotangent.dtype)
         gate_now = select_micro(gate_pre, micro_index)
         upward_now = select_micro(upward, micro_index)
         sigmoid_now = select_micro(gate_sigmoid, micro_index)

time: 1590 us -> 1590 us (level)
  no operation moved by 1% of the time
where the time goes in v1:
time: 1590 us
  waiting for transfers between devices  788 us (50%)
  matrix products  520 us (33%)
  blocking collectives  141 us (9%)
  other arithmetic  57.9 us (4%)
  local copies, waits for them, and re-layouts  52.2 us (3%)
    dot_general x27, matrix products, contract_rows(): lax.dot_general(left, right, (((0,), (0,)), ((), ())), preferred_element_...  381 us
    reduce_scatter x1, waiting for transfers between devices, shards(): lax.psum_scatter(stored[0], 'fsdp', scatter_dimension=0, tiled=True)  165 us
    reduce_scatter x1, waiting for transfers between devices, shards(): lax.psum_scatter(stored[2], 'fsdp', scatter_dimension=0, tiled=True)  165 us
    reduce_scatter x1, waiting for transfers between devices, shards(): lax.psum_scatter(stored[1], 'fsdp', scatter_dimension=0, tiled=True)  155 us
    all_gather x9, blocking collectives, jax.lax.all_gather(frame_in, 'tp')  132 us
    dot_general x27, matrix products, contract_cols(): lax.dot_general(left, right, (((1,), (1,)), ((), ())), preferred_element_...  121 us
    all_gather x1, waiting for transfers between devices, shards(): lax.all_gather(up_weight[0], 'fsdp', axis=0, tiled=True)  83.7 us
    all_gather x1, waiting for transfers between devices, shards(): lax.all_gather(gate_weight[0], 'fsdp', axis=0, tiled=True)  80.1 us
  transfers between devices with their start and end apart: 25, of which 17 were waited for; matrix products, arithmetic and copies ran while one was open for 29% of the time, Pallas kernels for 0%

profile of v1, /device:TPU:0, one launch (start us, length us, event | category | flops | bytes accessed | tf_op | source)
XLA Modules:
  0.0 1587.2 jit_solution(5817512145805291112)
XLA Ops:
  10.1 56.8 %all-gather.13.cloned.1.call-done = bf16[1,8,64,2560]{3,2,1,0:T(8,128)(2,1)} async-done(((bf16[1,8,64,640]{3,2,1,0:T(8,128)(2,1)}), bf16[1,8,64,2560]{3,2,1,0:T(8,128)(2,1)}) %all-gather.13.cloned.1.call-update) | async-done | bytes 2621456 | tf_op jit(solution)/shard_map/all_gather | solution.py:67
  75.1 83.7 %all-gather.17.cloned.1.call-done = bf16[1,2560,1728]{1,2,0:T(8,128)(2,1)} async-done(((bf16[1,640,1728]{1,2,0:T(8,128)(2,1)}), bf16[1,2560,1728]{1,2,0:T(8,128)(2,1)}) %all-gather.17.cloned.1.call-update) | async-done | bytes 8847376 | tf_op jit(solution)/shard_map/all_gather | solution.py:59
  158.8 13.1 copy.15
  171.8 80.1 %all-gather.19.cloned.1.call-done = bf16[1,2560,1728]{1,2,0:T(8,128)(2,1)} async-done(((bf16[1,640,1728]{1,2,0:T(8,128)(2,1)}), bf16[1,2560,1728]{1,2,0:T(8,128)(2,1)}) %all-gather.19.cloned.1.call-update) | async-done | bytes 8847376 | tf_op jit(solution)/shard_map/all_gather | solution.py:58
  251.9 13.1 copy.14
  274.4 11.5 multiply_convert_fusion.1
  285.9 59.1 %all-gather.15.cloned.1.call-done = bf16[1,1728,2560]{2,1,0:T(8,128)(2,1)} async-done(((bf16[1,1728,640]{2,1,0:T(8,128)(2,1)}), bf16[1,1728,2560]{2,1,0:T(8,128)(2,1)}) %all-gather.15.cloned.1.call-update) | async-done | bytes 8847376 | tf_op jit(solution)/shard_map/all_gather | solution.py:60
  345.9 738.7 %while.26 = (s32[]{:T(128)}, bf16[64,640]{1,0:T(8,128)(2,1)S(1)}, bf16[8,64,640]{2,1,0:T(8,128)(2,1)}, f32[640]{0:T(1024)S(1)}, f32[2560,1728]{0,1:T(8,128)}, /*...) while((s32[]{:T(128)}, bf16[64,640]{1,0:T(8,128)(2,1)S(1)}, ...), condition=%wide.region_5.6_spmd.clone, body=%wide.region_1.5_spmd.clone.sunk | while | flops 3426907392 | bytes 220313376 | solution.py:131
  346.8 14.2 all-gather.7
  385.9 9.6 select_add_fusion.11
  395.4 8.6 select_add_fusion.9
  404.0 12.9 all-reduce.2.cloned.1.call-done
  424.2 14.4 all-gather.7
  455.1 14.7 select_add_fusion.10
  469.8 14.9 select_add_fusion.11
  484.6 14.7 select_add_fusion.9
  506.7 14.3 all-gather.7
  537.4 14.7 select_add_fusion.10
  552.1 14.9 select_add_fusion.11
  566.9 14.7 select_add_fusion.9
  589.0 14.3 all-gather.7
  619.7 14.7 select_add_fusion.10
  634.4 14.9 select_add_fusion.11
  649.3 14.7 select_add_fusion.9
  671.3 14.3 all-gather.7
  702.0 14.7 select_add_fusion.10
  716.7 14.9 select_add_fusion.11
  731.6 14.7 select_add_fusion.9
  753.6 14.8 all-gather.7
  784.8 14.7 select_add_fusion.10
  799.5 14.9 select_add_fusion.11
  814.3 14.7 select_add_fusion.9
  836.4 15.1 all-gather.7
  867.8 14.7 select_add_fusion.10
  882.5 14.9 select_add_fusion.11
  897.4 14.7 select_add_fusion.9
  919.4 15.1 all-gather.7
  950.9 14.7 select_add_fusion.10
  965.5 14.9 select_add_fusion.11
  980.4 14.7 select_add_fusion.9
  1002.5 15.1 all-gather.7
  1033.9 14.7 select_add_fusion.10
  1048.6 14.9 select_add_fusion.11
  1063.5 14.7 select_add_fusion.9
  1086.3 9.8 psum.20
  1096.2 155.0 %reduce-scatter.6.cloned.1.call-done = f32[640,1728]{0,1:T(8,128)} async-done(((f32[2560,1728]{0,1:T(8,128)}), f32[640,1728]{0,1:T(8,128)}) %reduce-scatter.6.cloned.1.call-update) | async-done | bytes 4423696 | tf_op jit(solution)/shard_map/reduce_scatter | solution.py:136
  1251.1 164.8 %reduce-scatter.8.cloned.1.call-done = f32[640,1728]{0,1:T(8,128)} async-done(((f32[2560,1728]{0,1:T(8,128)}), f32[640,1728]{0,1:T(8,128)}) %reduce-scatter.8.cloned.1.call-update) | async-done | bytes 4423696 | tf_op jit(solution)/shard_map/reduce_scatter | solution.py:137
  1415.9 164.8 %reduce-scatter.4.cloned.1.call-done = f32[640,1728]{0,1:T(8,128)} async-done(((f32[2560,1728]{0,1:T(8,128)}), f32[640,1728]{0,1:T(8,128)}) %reduce-scatter.4.cloned.1.call-update) | async-done | bytes 4423696 | tf_op jit(solution)/shard_map/reduce_scatter | solution.py:135
  (277 shorter events, 243.8 us)
Async XLA Ops:
  7.2 59.7 %all-gather.13.cloned.1.call-start = ((), (), s32[]{:S(2)}) async-start(), calls=%async_computation.6 | async-start | bytes 3276800 | tf_op jit(solution)/shard_map/all_gather | solution.py:67
  7.9 150.8 %all-gather.17.cloned.1.call-start = ((), (), s32[]{:S(2)}) async-start(), calls=%async_computation.8 | async-start | bytes 11059200 | tf_op jit(solution)/shard_map/all_gather | solution.py:59
  8.7 243.3 %all-gather.19.cloned.1.call-start = ((), (), s32[]{:S(2)}) async-start(), calls=%async_computation.9 | async-start | bytes 11059200 | tf_op jit(solution)/shard_map/all_gather | solution.py:58
  9.4 335.6 %all-gather.15.cloned.1.call-start = ((), (), s32[]{:S(2)}) async-start(), calls=%async_computation.7 | async-start | bytes 11059200 | tf_op jit(solution)/shard_map/all_gather | solution.py:60
  66.9 4.9 copy-start.2
  345.9 71.0 %all-reduce.2.cloned.1.call-start = ((), (), s32[]{:S(2)}) async-start(), calls=%async_computation.10 | async-start | bytes 1310720 | tf_op jit(solution)/shard_map/while/body/eval_jaxpr/psum | solution.py:99
  361.3 6.9 copy-start
  395.4 23.0 %copy-start.3 = (bf16[1,64,640]{2,1,0:T(8,128)(2,1)S(1)}, bf16[1,64,640]{2,1,0:T(8,128)(2,1)}, u32[]{:S(2)}) copy-start(bf16[1,64,640]{2,1,0:T(8,128)(2,1)} %constant_dynamic-slice_fusion.3) | copy-start | bytes 245764 | tf_op jit(solution)/shard_map/while
  420.2 3.2 collective-permute-start
  423.3 76.0 %all-reduce.2.cloned.1.call-start = ((), (), s32[]{:S(2)}) async-start(), calls=%async_computation.10 | async-start | bytes 1310720 | tf_op jit(solution)/shard_map/while/body/eval_jaxpr/psum | solution.py:99
  439.0 6.9 copy-start
  445.8 3.6 copy-start.1
  484.6 16.2 %copy-start.3 = (bf16[1,64,640]{2,1,0:T(8,128)(2,1)S(1)}, bf16[1,64,640]{2,1,0:T(8,128)(2,1)}, u32[]{:S(2)}) copy-start(bf16[1,64,640]{2,1,0:T(8,128)(2,1)} %constant_dynamic-slice_fusion.3) | copy-start | bytes 245764 | tf_op jit(solution)/shard_map/while
  502.6 3.2 collective-permute-start
  505.8 75.9 %all-reduce.2.cloned.1.call-start = ((), (), s32[]{:S(2)}) async-start(), calls=%async_computation.10 | async-start | bytes 1310720 | tf_op jit(solution)/shard_map/while/body/eval_jaxpr/psum | solution.py:99
  521.3 6.9 copy-start
  528.2 3.6 copy-start.1
  566.9 16.2 %copy-start.3 = (bf16[1,64,640]{2,1,0:T(8,128)(2,1)S(1)}, bf16[1,64,640]{2,1,0:T(8,128)(2,1)}, u32[]{:S(2)}) copy-start(bf16[1,64,640]{2,1,0:T(8,128)(2,1)} %constant_dynamic-slice_fusion.3) | copy-start | bytes 245764 | tf_op jit(solution)/shard_map/while
  584.9 3.2 collective-permute-start
  588.1 75.9 %all-reduce.2.cloned.1.call-start = ((), (), s32[]{:S(2)}) async-start(), calls=%async_computation.10 | async-start | bytes 1310720 | tf_op jit(solution)/shard_map/while/body/eval_jaxpr/psum | solution.py:99
  603.6 6.9 copy-start
  649.3 16.2 %copy-start.3 = (bf16[1,64,640]{2,1,0:T(8,128)(2,1)S(1)}, bf16[1,64,640]{2,1,0:T(8,128)(2,1)}, u32[]{:S(2)}) copy-start(bf16[1,64,640]{2,1,0:T(8,128)(2,1)} %constant_dynamic-slice_fusion.3) | copy-start | bytes 245764 | tf_op jit(solution)/shard_map/while
  667.2 3.2 collective-permute-start
  670.4 75.9 %all-reduce.2.cloned.1.call-start = ((), (), s32[]{:S(2)}) async-start(), calls=%async_computation.10 | async-start | bytes 1310720 | tf_op jit(solution)/shard_map/while/body/eval_jaxpr/psum | solution.py:99
  685.9 6.9 copy-start
  731.6 16.2 %copy-start.3 = (bf16[1,64,640]{2,1,0:T(8,128)(2,1)S(1)}, bf16[1,64,640]{2,1,0:T(8,128)(2,1)}, u32[]{:S(2)}) copy-start(bf16[1,64,640]{2,1,0:T(8,128)(2,1)} %constant_dynamic-slice_fusion.3) | copy-start | bytes 245764 | tf_op jit(solution)/shard_map/while
  749.6 3.2 collective-permute-start
  752.7 76.3 %all-reduce.2.cloned.1.call-start = ((), (), s32[]{:S(2)}) async-start(), calls=%async_computation.10 | async-start | bytes 1310720 | tf_op jit(solution)/shard_map/while/body/eval_jaxpr/psum | solution.py:99
  768.7 6.9 copy-start
  814.3 16.2 %copy-start.3 = (bf16[1,64,640]{2,1,0:T(8,128)(2,1)S(1)}, bf16[1,64,640]{2,1,0:T(8,128)(2,1)}, u32[]{:S(2)}) copy-start(bf16[1,64,640]{2,1,0:T(8,128)(2,1)} %constant_dynamic-slice_fusion.3) | copy-start | bytes 245764 | tf_op jit(solution)/shard_map/while
  832.3 3.2 collective-permute-start
  835.5 76.6 %all-reduce.2.cloned.1.call-start = ((), (), s32[]{:S(2)}) async-start(), calls=%async_computation.10 | async-start | bytes 1310720 | tf_op jit(solution)/shard_map/while/body/eval_jaxpr/psum | solution.py:99
  851.7 6.9 copy-start
  858.6 3.6 copy-start.1
  897.4 16.2 %copy-start.3 = (bf16[1,64,640]{2,1,0:T(8,128)(2,1)S(1)}, bf16[1,64,640]{2,1,0:T(8,128)(2,1)}, u32[]{:S(2)}) copy-start(bf16[1,64,640]{2,1,0:T(8,128)(2,1)} %constant_dynamic-slice_fusion.3) | copy-start | bytes 245764 | tf_op jit(solution)/shard_map/while
  915.3 3.2 collective-permute-start
  918.5 76.6 %all-reduce.2.cloned.1.call-start = ((), (), s32[]{:S(2)}) async-start(), calls=%async_computation.10 | async-start | bytes 1310720 | tf_op jit(solution)/shard_map/while/body/eval_jaxpr/psum | solution.py:99
  934.8 6.9 copy-start
  980.4 16.2 %copy-start.3 = (bf16[1,64,640]{2,1,0:T(8,128)(2,1)S(1)}, bf16[1,64,640]{2,1,0:T(8,128)(2,1)}, u32[]{:S(2)}) copy-start(bf16[1,64,640]{2,1,0:T(8,128)(2,1)} %constant_dynamic-slice_fusion.3) | copy-start | bytes 245764 | tf_op jit(solution)/shard_map/while
  998.4 3.2 collective-permute-start
  1001.6 76.6 %all-reduce.2.cloned.1.call-start = ((), (), s32[]{:S(2)}) async-start(), calls=%async_computation.10 | async-start | bytes 1310720 | tf_op jit(solution)/shard_map/while/body/eval_jaxpr/psum | solution.py:99
  1017.8 6.9 copy-start
  1024.7 3.6 copy-start.1
  1063.5 16.2 %copy-start.3 = (bf16[1,64,640]{2,1,0:T(8,128)(2,1)S(1)}, bf16[1,64,640]{2,1,0:T(8,128)(2,1)}, u32[]{:S(2)}) copy-start(bf16[1,64,640]{2,1,0:T(8,128)(2,1)} %constant_dynamic-slice_fusion.3) | copy-start | bytes 245764 | tf_op jit(solution)/shard_map/while
  1081.4 3.2 collective-permute-start
  1084.6 166.6 %reduce-scatter.6.cloned.1.call-start = ((), (), s32[]{:S(2)}) async-start(), calls=%async_computation.4 | async-start | bytes 22118400 | tf_op jit(solution)/shard_map/reduce_scatter | solution.py:136
  1085.2 330.8 %reduce-scatter.8.cloned.1.call-start = ((), (), s32[]{:S(2)}) async-start(), calls=%async_computation.5 | async-start | bytes 22118400 | tf_op jit(solution)/shard_map/reduce_scatter | solution.py:137
  1085.8 494.9 %reduce-scatter.4.cloned.1.call-start = ((), (), s32[]{:S(2)}) async-start(), calls=%async_computation.3 | async-start | bytes 22118400 | tf_op jit(solution)/shard_map/reduce_scatter | solution.py:135
  (7 other events, 22.7 us)
Sparse Core Ops, SparseCore 0:
  9.6 57.2 all-gather.12
  68.7 89.9 all-gather.16
  160.6 91.2 all-gather.18
  253.6 91.2 all-gather.14
  375.6 41.2 all-reduce.1
  453.3 39.9 all-reduce.1
  535.6 40.3 all-reduce.1
  617.9 40.7 all-reduce.1
  700.2 41.3 all-reduce.1
  783.0 41.4 all-reduce.1
  866.0 41.4 all-reduce.1
  949.1 41.4 all-reduce.1
  1032.1 41.5 all-reduce.1
  1088.8 162.2 reduce-scatter.5
  1254.7 161.1 reduce-scatter.7
  1419.5 161.1 reduce-scatter.3
